TPU v7x, 128 devices: a whole 4x4x4 slice. The times are simulated.
128 devices in a mesh: dp: 1, tp: 2 (over core), sp: 64 (over z, y, x).
Axes of the slice: x: 4, y: 4, z: 4, core: 2. Of those that a mesh axis runs over, the one named last changes fastest.
Arguments:
- tok_emb: bfloat16 [4, 32, 1536], P(None, 'dp')
- lengths: int32 [32], P('dp')
- key_cache: bfloat16 [2, 32, 8192, 2, 128], P(None, 'dp', 'sp', 'tp')
- val_cache: bfloat16 [2, 32, 8192, 2, 128], P(None, 'dp', 'sp', 'tp')
- gain_attn: bfloat16 [2, 1536], replicated
- gain_mlp: bfloat16 [2, 1536], replicated
- w_query: bfloat16 [2, 1536, 1536], P(None, None, 'tp')
- w_key: bfloat16 [2, 1536, 256], P(None, None, 'tp')
- w_value: bfloat16 [2, 1536, 256], P(None, None, 'tp')
- w_out: bfloat16 [2, 1536, 1536], P(None, 'tp')
- w_gate: bfloat16 [2, 1536, 8960], P(None, None, 'tp')
- w_up: bfloat16 [2, 1536, 8960], P(None, None, 'tp')
- w_down: bfloat16 [2, 8960, 1536], P(None, 'tp')
Outputs:
- output 1: bfloat16 [4, 32, 1536], P(None, 'dp')
- output 2: bfloat16 [2, 32, 8192, 2, 128], P(None, 'dp', 'sp', 'tp')
- output 3: bfloat16 [2, 32, 8192, 2, 128], P(None, 'dp', 'sp', 'tp')
All inputs are finite; a program needn't handle non-finite values.
Results may differ from a plain program's by a relative error of at most 0.0151098.
Values sent between devices are 32-bit elements.
A program may use at most 1 GiB of HBM per device.

v0:
```python
import jax
import jax.numpy as jnp
from jax import lax
from jax.sharding import PartitionSpec as P

EPS = 1e-5
ROPE_BASE = 500000.0


def rms_norm(hidden, gain_vec):
    x_float = hidden.astype(jnp.float32)
    inv_rms = lax.rsqrt(jnp.mean(x_float * x_float, axis=-1, keepdims=True) + EPS)
    return (x_float * inv_rms * gain_vec.astype(jnp.float32)).astype(jnp.bfloat16)


def rotary(in_vecs, positions):
    head_dim = in_vecs.shape[-1]
    half_dim = head_dim // 2
    inv_freq = 1.0 / (ROPE_BASE ** (jnp.arange(half_dim).astype(jnp.float32) * 2.0 / head_dim))
    angles = positions.astype(jnp.float32)[:, None] * inv_freq[None, :]
    cos_a = jnp.cos(angles)[:, None, :]
    sin_a = jnp.sin(angles)[:, None, :]
    front_half = in_vecs[..., :half_dim]
    back_half = in_vecs[..., half_dim:]
    return jnp.concatenate([front_half * cos_a - back_half * sin_a, back_half * cos_a + front_half * sin_a], axis=-1)


def project(normed, weight):
    return jnp.dot(normed, weight, preferred_element_type=jnp.float32)


def solution(mesh):
    sp_size = mesh.shape['sp']

    def local_fn(tok_emb, lengths, key_cache, val_cache, gain_attn, gain_mlp, w_query, w_key, w_value, w_out, w_gate, w_up, w_down):
        n_steps, n_batch, _ = tok_emb.shape
        n_layers, _, loc_len, kv_loc, head_dim = key_cache.shape
        heads_loc = w_query.shape[2] // head_dim
        group_size = heads_loc // kv_loc
        my_sp = lax.axis_index('sp')
        slot_pos = jnp.arange(loc_len) * sp_size + my_sp
        row_ids = jnp.arange(n_batch)
        new_keys = key_cache
        new_vals = val_cache
        hidden_list = []
        for step_idx in range(n_steps):
            cur_pos = lengths + step_idx
            write_slot = jnp.where(cur_pos % sp_size == my_sp, cur_pos // sp_size, loc_len)
            valid_mask = (slot_pos[None, :] <= cur_pos[:, None])[:, None, None, :]
            hidden = tok_emb[step_idx]
            for layer_idx in range(n_layers):
                normed = rms_norm(hidden, gain_attn[layer_idx])
                q_vec = project(normed, w_query[layer_idx]).reshape(n_batch, heads_loc, head_dim)
                k_vec = project(normed, w_key[layer_idx]).reshape(n_batch, kv_loc, head_dim)
                v_vec = project(normed, w_value[layer_idx]).reshape(n_batch, kv_loc, head_dim).astype(jnp.bfloat16)
                q_rot = rotary(q_vec, cur_pos).astype(jnp.bfloat16).reshape(n_batch, kv_loc, group_size, head_dim)
                k_rot = rotary(k_vec, cur_pos).astype(jnp.bfloat16)
                new_keys = new_keys.at[layer_idx, row_ids, write_slot].set(k_rot, mode='drop')
                new_vals = new_vals.at[layer_idx, row_ids, write_slot].set(v_vec, mode='drop')
                scores = jnp.einsum('bkgd,bjkd->bkgj', q_rot, new_keys[layer_idx], preferred_element_type=jnp.float32) * head_dim ** -0.5
                scores = jnp.where(valid_mask, scores, -1e30)
                loc_max = jnp.max(scores, axis=-1, keepdims=True)
                prob_w = jnp.exp(scores - loc_max)
                loc_sum = jnp.sum(prob_w, axis=-1, keepdims=True)
                loc_out = jnp.einsum('bkgj,bjkd->bkgd', prob_w.astype(jnp.bfloat16), new_vals[layer_idx], preferred_element_type=jnp.float32)
                glob_max = lax.pmax(loc_max, 'sp')
                rescale = jnp.exp(loc_max - glob_max)
                merged = lax.psum(jnp.concatenate([loc_out, loc_sum], axis=-1) * rescale, 'sp')
                attn_out = (merged[..., :head_dim] / merged[..., head_dim:]).astype(jnp.bfloat16).reshape(n_batch, heads_loc * head_dim)
                proj_sum = lax.psum(project(attn_out, w_out[layer_idx]), 'tp')
                hidden = (hidden.astype(jnp.float32) + proj_sum).astype(jnp.bfloat16)
                normed = rms_norm(hidden, gain_mlp[layer_idx])
                mlp_act = (jax.nn.silu(project(normed, w_gate[layer_idx])) * project(normed, w_up[layer_idx])).astype(jnp.bfloat16)
                down_sum = lax.psum(project(mlp_act, w_down[layer_idx]), 'tp')
                hidden = (hidden.astype(jnp.float32) + down_sum).astype(jnp.bfloat16)
            hidden_list.append(hidden)
        return jnp.stack(hidden_list), new_keys, new_vals

    cache_spec = P(None, 'dp', 'sp', 'tp', None)
    col_spec = P(None, None, 'tp')
    row_spec = P(None, 'tp', None)
    emb_spec = P(None, 'dp', None)
    return jax.shard_map(local_fn, mesh=mesh, in_specs=(emb_spec, P('dp'), cache_spec, cache_spec, P(), P(), col_spec, col_spec, col_spec, row_spec, col_spec, col_spec, row_spec), out_specs=(emb_spec, cache_spec, cache_spec), check_vma=False)
```

profile of v0, /device:TPU:1, one launch (start us, length us, event | category | flops | bytes accessed | tf_op | source)
XLA Modules:
  0.0 2955.6 jit_solution(298896290182285897)
XLA Ops:
  7.2 3.3 copy.246
  16.0 4.8 slice_bitcast_fusion
  20.8 2.8 copy.64
  25.9 4.1 scatter_fusion
  32.6 295.6 %pmax.56 = f32[32,1,6,1]{2,0,3,1:T(8,128)S(1)} all-reduce(f32[32,1,6,1]{2,0,3,1:T(8,128)S(1)} %bitcast.565), channel_id=1, replica_groups=mesh['dp'=1,'tp'=2,'sp'=64] {'sp'}, use_global_device_ids=true, to_apply=%region_5.6 | all-reduce | flops 192 | bytes 1536 | tf_op jit(solution)/shard_map/pmax | solution.py:66
  328.4 4.1 scatter_fusion.1
  336.8 2.8 copy.70
  343.4 167.2 %all-reduce.20.cloned.1.call-done = f32[32,1,6,129]{3,2,0,1:T(8,128)} async-done(((f32[32,1,6,129]{3,2,0,1:T(8,128)}), f32[32,1,6,129]{3,2,0,1:T(8,128)}) %all-reduce.20.cloned.1.call-update) | async-done | bytes 99088 | tf_op jit(solution)/shard_map/psum | solution.py:68
  512.8 2.9 fusion.134
  517.0 22.7 all-reduce.22.cloned.1.call-done
  540.7 7.1 fusion.46
  547.8 12.3 fusion.30
  561.1 24.0 all-reduce.24.cloned.1.call-done
  588.8 4.1 scatter_fusion.3
  593.0 4.1 scatter_fusion.2
  599.4 4.1 scatter_fusion.4
  605.4 293.5 %pmax.58 = f32[32,1,6,1]{2,0,3,1:T(8,128)S(1)} all-reduce(f32[32,1,6,1]{2,0,3,1:T(8,128)S(1)} %bitcast.562), channel_id=1, replica_groups=mesh['dp'=1,'tp'=2,'sp'=64] {'sp'}, use_global_device_ids=true, to_apply=%region_25.26 | all-reduce | flops 192 | bytes 1536 | tf_op jit(solution)/shard_map/pmax | solution.py:66
  901.4 4.1 scatter_fusion.5
  909.7 173.2 %all-reduce.26.cloned.1.call-done = f32[32,1,6,129]{3,2,0,1:T(8,128)} async-done(((f32[32,1,6,129]{3,2,0,1:T(8,128)}), f32[32,1,6,129]{3,2,0,1:T(8,128)}) %all-reduce.26.cloned.1.call-update) | async-done | bytes 99088 | tf_op jit(solution)/shard_map/psum | solution.py:68
  1085.1 2.9 fusion.132
  1090.0 21.9 all-reduce.28.cloned.1.call-done
  1113.0 7.1 fusion.44
  1120.1 12.3 fusion.28
  1134.7 22.6 all-reduce.30.cloned.1.call-done
  1161.7 4.1 scatter_fusion.7
  1166.8 4.1 scatter_fusion.6
  1173.1 3.7 scatter_fusion.8
  1178.8 293.0 %pmax.60 = f32[32,1,6,1]{2,0,3,1:T(8,128)S(1)} all-reduce(f32[32,1,6,1]{2,0,3,1:T(8,128)S(1)} %bitcast.563), channel_id=1, replica_groups=mesh['dp'=1,'tp'=2,'sp'=64] {'sp'}, use_global_device_ids=true, to_apply=%region_45.46 | all-reduce | flops 192 | bytes 1536 | tf_op jit(solution)/shard_map/pmax | solution.py:66
  1475.0 3.7 scatter_fusion.9
  1485.0 172.6 %all-reduce.32.cloned.1.call-done = f32[32,1,6,129]{3,2,0,1:T(8,128)} async-done(((f32[32,1,6,129]{3,2,0,1:T(8,128)}), f32[32,1,6,129]{3,2,0,1:T(8,128)}) %all-reduce.32.cloned.1.call-update) | async-done | bytes 99088 | tf_op jit(solution)/shard_map/psum | solution.py:68
  1659.8 2.9 fusion.130
  1663.5 23.1 all-reduce.34.cloned.1.call-done
  1687.7 7.1 fusion.42
  1694.8 12.3 fusion.26
  1708.2 23.9 all-reduce.36.cloned.1.call-done
  1736.7 3.7 scatter_fusion.11
  1740.5 3.7 scatter_fusion.10
  1746.4 3.7 scatter_fusion.12
  1752.0 294.2 %pmax.62 = f32[32,1,6,1]{2,0,3,1:T(8,128)} all-reduce(f32[32,1,6,1]{2,0,3,1:T(8,128)S(1)} %bitcast.564), channel_id=1, replica_groups=mesh['dp'=1,'tp'=2,'sp'=64] {'sp'}, use_global_device_ids=true, to_apply=%region_65.66 | all-reduce | flops 192 | bytes 1536 | tf_op jit(solution)/shard_map/pmax | solution.py:66
  2050.7 3.7 scatter_fusion.13
  2059.5 174.4 %all-reduce.38.cloned.1.call-done = f32[32,1,6,129]{3,2,0,1:T(8,128)} async-done(((f32[32,1,6,129]{3,2,0,1:T(8,128)}), f32[32,1,6,129]{3,2,0,1:T(8,128)}) %all-reduce.38.cloned.1.call-update) | async-done | bytes 99088 | tf_op jit(solution)/shard_map/psum | solution.py:68
  2236.2 2.9 fusion.128
  2239.6 23.4 all-reduce.40.cloned.1.call-done
  2264.1 7.1 fusion.40
  2271.2 12.3 fusion.24
  2284.8 23.7 all-reduce.42.cloned.1.call-done
  2311.4 3.7 scatter_fusion.15
  2315.2 3.7 scatter_fusion.14
  2322.8 294.6 %all-reduce.1 = (f32[32,1,6,1]{2,0,3,1:T(8,128)S(1)}, f32[32,1,6,1]{2,0,3,1:T(8,128)S(1)}, f32[32,1,6,1]{2,0,3,1:T(8,128)S(1)}, f32[32,1,6,1]{2,0,3,1:T(8,128)S(1)}) all-reduce(f32[32,1,6,1]{2,0,3,1:T(8,128)S(1)} %bitcast.569, f32[32,1,6,1]{2,0,3,1:T(8,128)S(1)} %bitcast.568, ...), channel_id=1, replica_groups=mesh['dp'=1,'tp'=2,'sp'=64] {'sp'}, use_global_device_ids=true, to_apply=%region_75.76 | all-reduce | flops 768 | bytes 6144 | tf_op jit(solution)/shard_map/pmax | solution.py:66
  2621.1 179.4 %all-reduce.44.cloned.1.call-done = (f32[32,1,6,129]{3,2,0,1:T(8,128)}, f32[32,1,6,129]{3,2,0,1:T(8,128)}, f32[32,1,6,129]{3,2,0,1:T(8,128)}, f32[32,1,6,129]{3,2,0,1:T(8,128)}) async-done(((f32[32,1,6,129]{3,2,0,1:T(8,128)}, f32[32,1,6,129]{3,2,0,1:T(8,128)}, f32[32,1,6,129]{3,2,0,1:T(8,128)}, f32[32,1,6,129]{3,2,0,1:T(8,128)}), (f32[32,1,6,129]{3,2,0,1:T(8,128)}, f32[32,1,6,129]{3,2,0,1:T(8,128)}, ...) | async-done | bytes 396304 | tf_op jit(solution)/shard_map/psum | solution.py:68
  2802.8 2.9 fusion.120
  2806.1 2.9 fusion.122
  2809.4 2.9 fusion.124
  2812.7 2.9 fusion.126
  2815.9 24.0 all-reduce.48.cloned.1.call-done
  2844.2 6.3 fusion.22
  2850.6 12.1 fusion.6
  2862.7 6.3 fusion.20
  2869.0 12.1 fusion.4
  2881.1 6.3 fusion.18
  2887.4 12.1 fusion.2
  2899.6 6.3 fusion.16
  2905.9 12.1 fusion
  2918.0 26.0 all-reduce.46.cloned.1.call-done
  (333 shorter events, 116.6 us)
Async XLA Ops:
  7.2 503.4 %all-reduce.20.cloned.1.call-start = ((), (), s32[]{:S(2)}) async-start(), calls=%async_computation | async-start | bytes 524288 | tf_op jit(solution)/shard_map/psum | solution.py:68
  11.9 12.9 copy-start.39
  11.9 12.8 copy-start.44
  12.0 12.8 copy-start.47
  12.0 12.8 copy-start.50
  12.0 12.8 copy-start.52
  14.8 327.5 %copy-start.61 = (f32[32]{0:T(128)}, f32[32]{0:T(128)S(1)}, u32[]{:S(2)}) copy-start(f32[32]{0:T(128)S(1)} %get-tuple-element.149) | copy-start | bytes 388
  23.7 311.7 %copy-start = (bf16[768,1536]{1,0:T(8,128)(2,1)}, bf16[768,1536]{1,0:T(8,128)(2,1)S(1)}, u32[]{:S(2)}) copy-start(bf16[768,1536]{1,0:T(8,128)(2,1)S(1)} %copy.64) | copy-start | bytes 7077892
  25.7 317.4 %copy-start.26 = (f32[32,64]{1,0:T(8,128)}, f32[32,64]{1,0:T(8,128)S(1)}, u32[]{:S(2)}) copy-start(f32[32,64]{1,0:T(8,128)S(1)} %get-tuple-element.113) | copy-start | bytes 24580
  25.7 317.4 %copy-start.28 = (f32[32,64]{1,0:T(8,128)}, f32[32,64]{1,0:T(8,128)S(1)}, u32[]{:S(2)}) copy-start(f32[32,64]{1,0:T(8,128)S(1)} %get-tuple-element.114) | copy-start | bytes 24580
  25.7 534.7 %copy-start.22 = (f32[32,64]{1,0:T(8,128)}, f32[32,64]{1,0:T(8,128)S(1)}, u32[]{:S(2)}) copy-start(f32[32,64]{1,0:T(8,128)S(1)} %get-tuple-element.115) | copy-start | bytes 24580
  25.7 534.7 %copy-start.24 = (f32[32,64]{1,0:T(8,128)}, f32[32,64]{1,0:T(8,128)S(1)}, u32[]{:S(2)}) copy-start(f32[32,64]{1,0:T(8,128)S(1)} %get-tuple-element.116) | copy-start | bytes 24580
  30.6 297.7 %copy-start.33 = (pred[32,128]{1,0:T(8,128)(4,1)}, pred[32,128]{1,0:T(8,128)(4,1)S(1)}, u32[]{:S(2)}) copy-start(pred[32,128]{1,0:T(8,128)(4,1)S(1)} %get-tuple-element.105) | copy-start | bytes 12292
  30.6 1146.2 %copy-start.31 = (pred[32,128]{1,0:T(8,128)(4,1)}, pred[32,128]{1,0:T(8,128)(4,1)S(1)}, u32[]{:S(2)}) copy-start(pred[32,128]{1,0:T(8,128)(4,1)S(1)} %get-tuple-element.104) | copy-start | bytes 12292
  335.3 204.4 %all-reduce.22.cloned.1.call-start = ((), (), s32[]{:S(2)}) async-start(), calls=%async_computation.1 | async-start | bytes 393216 | tf_op jit(solution)/shard_map/psum | solution.py:70
  336.8 211.0 %copy-start.55 = (f32[1536]{0:T(1024)}, f32[1536]{0:T(1024)S(1)}, u32[]{:S(2)}) copy-start(f32[1536]{0:T(1024)S(1)} %get-tuple-element.17) | copy-start | bytes 18436
  515.7 69.4 %all-reduce.24.cloned.1.call-start = ((), (), s32[]{:S(2)}) async-start(), calls=%async_computation.2 | async-start | bytes 393216 | tf_op jit(solution)/shard_map/psum | solution.py:74
  547.8 40.9 %copy-start.40 = (f32[64]{0:T(128)S(1)}, f32[64]{0:T(128)}, u32[]{:S(2)}) copy-start(f32[64]{0:T(128)} %copy-done.39) | copy-start | bytes 772
  547.8 40.9 %copy-start.53 = (f32[32]{0:T(128)S(1)}, f32[32]{0:T(128)}, u32[]{:S(2)}) copy-start(f32[32]{0:T(128)} %copy-done.52) | copy-start | bytes 388
  560.1 522.8 %all-reduce.26.cloned.1.call-start = ((), (), s32[]{:S(2)}) async-start(), calls=%async_computation.3 | async-start | bytes 524288 | tf_op jit(solution)/shard_map/psum | solution.py:68
  586.2 11.9 copy-start.34
  603.5 304.9 %copy-start.62 = (f32[32]{0:T(128)S(1)}, f32[32]{0:T(128)}, u32[]{:S(2)}) copy-start(f32[32]{0:T(128)} %copy-done.61) | copy-start | bytes 388
  908.3 179.7 %copy-start.14 = (bf16[32,6,64]{2,0,1:T(8,128)(2,1)S(1)}, bf16[32,6,64]{2,0,1:T(8,128)(2,1)}, u32[]{:S(2)}) copy-start(bf16[32,6,64]{2,0,1:T(8,128)(2,1)} %get-tuple-element.72) | copy-start | bytes 73732
  908.3 179.7 %copy-start.15 = (bf16[32,6,64]{2,0,1:T(8,128)(2,1)S(1)}, bf16[32,6,64]{2,0,1:T(8,128)(2,1)}, u32[]{:S(2)}) copy-start(bf16[32,6,64]{2,0,1:T(8,128)(2,1)} %get-tuple-element.73) | copy-start | bytes 73732
  908.3 180.4 %copy-start.64 = (f32[32]{0:T(128)S(1)}, f32[32]{0:T(128)}, u32[]{:S(2)}) copy-start(f32[32]{0:T(128)} %copy-done.63) | copy-start | bytes 388
  908.4 203.5 %all-reduce.28.cloned.1.call-start = ((), (), s32[]{:S(2)}) async-start(), calls=%async_computation.4 | async-start | bytes 393216 | tf_op jit(solution)/shard_map/psum | solution.py:70
  909.7 203.3 %copy-start.56 = (f32[1536]{0:T(1024)S(1)}, f32[1536]{0:T(1024)}, u32[]{:S(2)}) copy-start(f32[1536]{0:T(1024)} %copy-done.55) | copy-start | bytes 18436
  1088.0 69.4 %all-reduce.30.cloned.1.call-start = ((), (), s32[]{:S(2)}) async-start(), calls=%async_computation.5 | async-start | bytes 393216 | tf_op jit(solution)/shard_map/psum | solution.py:74
  1132.4 33.5 %copy-start.41 = (f32[64]{0:T(128)S(1)}, f32[64]{0:T(128)}, u32[]{:S(2)}) copy-start(f32[64]{0:T(128)} %copy-done.39) | copy-start | bytes 772
  1132.4 33.5 %copy-start.45 = (f32[32]{0:T(128)S(1)}, f32[32]{0:T(128)}, u32[]{:S(2)}) copy-start(f32[32]{0:T(128)} %copy-done.44) | copy-start | bytes 388
  1132.4 33.5 %copy-start.48 = (f32[32]{0:T(128)S(1)}, f32[32]{0:T(128)}, u32[]{:S(2)}) copy-start(f32[32]{0:T(128)} %copy-done.47) | copy-start | bytes 388
  1132.4 33.5 %copy-start.51 = (f32[32]{0:T(128)S(1)}, f32[32]{0:T(128)}, u32[]{:S(2)}) copy-start(f32[32]{0:T(128)} %copy-done.50) | copy-start | bytes 388
  1132.4 525.1 %all-reduce.32.cloned.1.call-start = ((), (), s32[]{:S(2)}) async-start(), calls=%async_computation.6 | async-start | bytes 524288 | tf_op jit(solution)/shard_map/psum | solution.py:68
  1134.7 36.2 %copy-start.27 = (f32[32,64]{1,0:T(8,128)S(1)}, f32[32,64]{1,0:T(8,128)}, u32[]{:S(2)}) copy-start(f32[32,64]{1,0:T(8,128)} %copy-done.26) | copy-start | bytes 24580
  1134.7 36.2 %copy-start.29 = (f32[32,64]{1,0:T(8,128)S(1)}, f32[32,64]{1,0:T(8,128)}, u32[]{:S(2)}) copy-start(f32[32,64]{1,0:T(8,128)} %copy-done.28) | copy-start | bytes 24580
  1176.8 306.3 %copy-start.65 = (f32[32]{0:T(128)S(1)}, f32[32]{0:T(128)}, u32[]{:S(2)}) copy-start(f32[32]{0:T(128)} %copy-done.63) | copy-start | bytes 388
  1481.3 181.4 %copy-start.18 = (f32[32,64]{1,0:T(8,128)S(1)}, f32[32,64]{1,0:T(8,128)}, u32[]{:S(2)}) copy-start(f32[32,64]{1,0:T(8,128)} %get-tuple-element.94) | copy-start | bytes 24580
  1481.3 181.4 %copy-start.20 = (f32[32,64]{1,0:T(8,128)S(1)}, f32[32,64]{1,0:T(8,128)}, u32[]{:S(2)}) copy-start(f32[32,64]{1,0:T(8,128)} %get-tuple-element.95) | copy-start | bytes 24580
  1483.1 204.6 %copy-start.57 = (f32[1536]{0:T(1024)S(1)}, f32[1536]{0:T(1024)}, u32[]{:S(2)}) copy-start(f32[1536]{0:T(1024)} %copy-done.55) | copy-start | bytes 18436
  1483.1 203.5 %all-reduce.34.cloned.1.call-start = ((), (), s32[]{:S(2)}) async-start(), calls=%async_computation.7 | async-start | bytes 393216 | tf_op jit(solution)/shard_map/psum | solution.py:70
  1662.7 69.5 %all-reduce.36.cloned.1.call-start = ((), (), s32[]{:S(2)}) async-start(), calls=%async_computation.8 | async-start | bytes 393216 | tf_op jit(solution)/shard_map/psum | solution.py:74
  1694.8 12.6 copy-start.16
  1694.8 12.6 copy-start.17
  1694.8 13.3 copy-start.35
  1694.8 13.3 copy-start.36
  1707.1 29.4 copy-start.42
  1707.1 29.4 copy-start.49
  1707.2 526.8 %all-reduce.38.cloned.1.call-start = ((), (), s32[]{:S(2)}) async-start(), calls=%async_computation.9 | async-start | bytes 524288 | tf_op jit(solution)/shard_map/psum | solution.py:68
  1707.4 36.8 %copy-start.23 = (f32[32,64]{1,0:T(8,128)S(1)}, f32[32,64]{1,0:T(8,128)}, u32[]{:S(2)}) copy-start(f32[32,64]{1,0:T(8,128)} %copy-done.22) | copy-start | bytes 24580
  1707.4 36.8 %copy-start.25 = (f32[32,64]{1,0:T(8,128)S(1)}, f32[32,64]{1,0:T(8,128)}, u32[]{:S(2)}) copy-start(f32[32,64]{1,0:T(8,128)} %copy-done.24) | copy-start | bytes 24580
  2059.5 203.5 %all-reduce.40.cloned.1.call-start = ((), (), s32[]{:S(2)}) async-start(), calls=%async_computation.10 | async-start | bytes 393216 | tf_op jit(solution)/shard_map/psum | solution.py:70
  2239.1 69.5 %all-reduce.42.cloned.1.call-start = ((), (), s32[]{:S(2)}) async-start(), calls=%async_computation.11 | async-start | bytes 393216 | tf_op jit(solution)/shard_map/psum | solution.py:74
  2283.5 27.6 copy-start.19
  2283.5 27.6 copy-start.21
  2283.6 516.9 %all-reduce.44.cloned.1.call-start = ((), (), s32[]{:S(2)}) async-start(), calls=%async_computation.12 | async-start | bytes 2097152 | tf_op jit(solution)/shard_map/psum | solution.py:68
  2284.3 26.9 copy-start.43
  2284.3 26.9 copy-start.46
  2310.9 307.0 %copy-start.7 = (f32[32,1,6,128]{3,2,0,1:T(8,128)S(1)}, f32[32,1,6,128]{3,2,0,1:T(8,128)}, u32[]{:S(2)}) copy-start(f32[32,1,6,128]{3,2,0,1:T(8,128)} %convolution_bitcast_fusion.6) | copy-start | bytes 294916
  2311.1 307.5 %copy-start.8 = (f32[32,1,6,128]{3,2,0,1:T(8,128)S(1)}, f32[32,1,6,128]{3,2,0,1:T(8,128)}, u32[]{:S(2)}) copy-start(f32[32,1,6,128]{3,2,0,1:T(8,128)} %convolution_bitcast_fusion.4) | copy-start | bytes 294916
  2311.4 308.0 %copy-start.9 = (f32[32,1,6,128]{3,2,0,1:T(8,128)S(1)}, f32[32,1,6,128]{3,2,0,1:T(8,128)}, u32[]{:S(2)}) copy-start(f32[32,1,6,128]{3,2,0,1:T(8,128)} %convolution_bitcast_fusion.2) | copy-start | bytes 294916
  2621.1 218.8 %all-reduce.48.cloned.1.call-start = ((), (), s32[]{:S(2)}) async-start(), calls=%async_computation.14 | async-start | bytes 1572864 | tf_op jit(solution)/shard_map/psum | solution.py:70
  2812.3 28.7 copy-start.6
  2812.7 31.5 %copy-start.54 = (f32[1536]{0:T(1024)S(1)}, f32[1536]{0:T(1024)}, u32[]{:S(2)}) copy-start(f32[1536]{0:T(1024)} %get-tuple-element.16) | copy-start | bytes 18436
  2815.6 128.5 %all-reduce.46.cloned.1.call-start = ((), (), s32[]{:S(2)}) async-start(), calls=%async_computation.13 | async-start | bytes 1572864 | tf_op jit(solution)/shard_map/psum | solution.py:74
  (19 other events, 94.1 us)
Sparse Core Ops, SparseCore 0:
  335.4 175.1 all-reduce.19
  515.8 23.7 all-reduce.21
  560.2 24.8 all-reduce.23
  908.5 174.3 all-reduce.25
  1088.1 23.7 all-reduce.27
  1132.5 24.8 all-reduce.29
  1483.2 174.3 all-reduce.31
  1662.8 23.7 all-reduce.33
  1707.3 24.8 all-reduce.35
  2059.6 174.2 all-reduce.37
  2239.2 23.7 all-reduce.39
  2283.7 24.8 all-reduce.41
  2621.2 179.2 all-reduce.43
  2815.7 24.0 all-reduce.47
  2918.2 25.8 all-reduce.45
where the time goes:
time: 2970 us; the launch traced here: 2960 us
  blocking collectives  1470 us (49%)
  waiting for transfers between devices  1100 us (37%)
  matrix products  232 us (8%)
  local copies, waits for them, and re-layouts  88.5 us (3%)
  other arithmetic  44.1 us (1%)
    pmax x5, blocking collectives, local_fn(): glob_max = lax.pmax(loc_max, 'sp')  1470 us
    psum x5, waiting for transfers between devices, local_fn(): lax.psum(jnp.concatenate([loc_out, loc_sum], axis=-1) * rescale, 'sp')  867 us
    dot_general x48, matrix products, project(): return jnp.dot(normed, weight, preferred_element_type=jnp.float32)  201 us
    psum x5, waiting for transfers between devices, local_fn(): down_sum = lax.psum(project(mlp_act, w_down[layer_idx]), 'tp')  120 us
    psum x5, waiting for transfers between devices, local_fn(): proj_sum = lax.psum(project(attn_out, w_out[layer_idx]), 'tp')  115 us
  transfers between devices with their start and end apart: 15, of which 15 were waited for; matrix products, arithmetic and copies ran while one was open for 1% of the time, Pallas kernels for 0%

commit v1 on v0

v1 whole, which is shorter than its diff:
```python
import functools
import jax
import jax.numpy as jnp
from jax import lax
from jax.experimental import pallas as pl
from jax.experimental.pallas import tpu as pltpu
from jax.sharding import PartitionSpec as P

EPS = 1e-5
ROPE_BASE = 500000.0
F32 = jnp.float32
BF16 = jnp.bfloat16
MESH = pl.DeviceIdType.MESH
LANES = 128
MLP_CHUNK = 1280
SEQ_UNROLL = 4


def rms_norm(x, gain):
    inv_rms = lax.rsqrt(jnp.mean(x * x, axis=-1, keepdims=True) + EPS)
    return (x * inv_rms * gain.astype(F32)).astype(BF16)


def dot(a, b):
    return jnp.dot(a, b, preferred_element_type=F32)


def decode_kernel(cfg, emb, kc, vc, wq, wk, wv, wo, wg, wu, wd, cos_ref, sin_ref, lim_ref, wsl_ref, slot_ref, ga, gm,
                  out, ksel_out, vsel_out,
                  emb_v, k_v, v_v, wqkv_v, wo_v, wg_v, wu_v, wd_v, u3, qtmp, qs, limr, ktok, vtok, ksel, vsel,
                  send, recv, pad_a, res, g_v, acc, xs, xr, ag, ubuf,
                  in_sem, kv_sem, qkv_sem, wo_sem, g_sem, u_sem, d_sem,
                  rs_ss, rs_rs, x_ss, x_rs, ag_ss, ag_rs, dd_ss, dd_rs):
    dims, n_steps, n_layers, n_seq, heads, d_model, ff = cfg
    nz, ny, nx = dims
    n_sp = nz * ny * nx
    n_tok = n_steps * n_seq
    blocks = d_model // LANES
    q_cols = heads * LANES
    chunk = min(MLP_CHUNK, ff)
    n_full, tail = ff // chunk, ff % chunk
    me = lax.axis_index('sp')
    core = lax.axis_index('tp')
    other = 1 - core
    start_row = lax.rem(me // (ny * nx) + nz // 2, nz) * ny + lax.rem(lax.rem(me // nx, ny) + ny // 2, ny)
    start_seq = start_row * (nx // 2)

    def at_sp(dst):
        return {'sp': dst}

    barrier = pltpu.get_barrier_semaphore()

    def hello(i, carry):
        peer = lax.rem(me + i, n_sp)
        pl.semaphore_signal(barrier, inc=1, device_id=at_sp(peer), device_id_type=MESH)
        return carry

    lax.fori_loop(1, n_sp, hello, 0)
    pl.semaphore_signal(barrier, inc=1, device_id={'tp': other}, device_id_type=MESH)

    def qkv_copies(layer):
        return [
            pltpu.make_async_copy(wq.at[layer], wqkv_v.at[:, pl.ds(0, q_cols)], qkv_sem.at[0]),
            pltpu.make_async_copy(wk.at[layer], wqkv_v.at[:, pl.ds(q_cols, LANES)], qkv_sem.at[1]),
            pltpu.make_async_copy(wv.at[layer], wqkv_v.at[:, pl.ds(q_cols + LANES, LANES)], qkv_sem.at[2]),
        ]

    def kv_copies(layer):
        return [
            pltpu.make_async_copy(kc.at[layer], k_v.at[layer], kv_sem.at[layer, 0]),
            pltpu.make_async_copy(vc.at[layer], v_v.at[layer], kv_sem.at[layer, 1]),
        ]

    def wo_copy(layer):
        return pltpu.make_async_copy(wo.at[layer], wo_v, wo_sem)

    def cols_copy(hbm, vmem, sem, layer, c, size):
        cols = pl.ds(pl.multiple_of(c * chunk, LANES), size)
        return pltpu.make_async_copy(hbm.at[layer, :, cols], vmem.at[:, cols], sem.at[c])

    def rows_copy(layer, c, size):
        rows = pl.ds(pl.multiple_of(c * chunk, LANES), size)
        return pltpu.make_async_copy(wd.at[layer, rows, :], wd_v.at[rows, :], d_sem.at[c])

    pieces = [(c, chunk) for c in range(n_full)] + ([(n_full, tail)] if tail else [])

    emb_copy = pltpu.make_async_copy(emb, emb_v, in_sem)
    emb_copy.start()
    for copy in qkv_copies(0) + kv_copies(0):
        copy.start()
    wo_copy(0).start()
    for c, size in pieces:
        cols_copy(wg, wg_v, g_sem, 0, c, size).start()
        cols_copy(wu, wu_v, u_sem, 0, c, size).start()
    for c, size in pieces:
        rows_copy(0, c, size).start()
    for copy in kv_copies(1):
        copy.start()

    for r in range(8):
        limr[pl.ds(r, n_tok, stride=8), :] = lim_ref[...]
    zeros = jnp.zeros((n_tok, LANES), F32)
    for r in range(heads, 8):
        qs[pl.ds(r, n_tok, stride=8), :] = zeros
    pad_a[...] = jnp.zeros_like(pad_a)
    res[...] = jnp.zeros_like(res)

    emb_copy.wait()
    for s in range(n_steps):
        for j in range(blocks):
            u3[j, pl.ds(s, n_seq, stride=n_steps), :] = emb_v[s, :, j * LANES:(j + 1) * LANES].astype(F32)
    for t in range(2):
        for j in range(blocks):
            res[t:t + 1, j * LANES:(j + 1) * LANES] = u3[j, pl.ds(2 * me + t, 1), :]

    def exchange(layer, phase, part):
        xs[layer, phase] = part
        copy = pltpu.make_async_remote_copy(
            src_ref=xs.at[layer, phase], dst_ref=xr.at[layer, phase], send_sem=x_ss.at[layer, phase], recv_sem=x_rs.at[layer, phase],
            device_id={'tp': other}, device_id_type=MESH)
        copy.start()
        copy.wait()
        return part + xr[layer, phase]

    for layer in range(n_layers):
        x = jnp.concatenate([u3[j] for j in range(blocks)], axis=-1)
        normed = rms_norm(x, ga[layer:layer + 1, :])
        for copy in qkv_copies(layer):
            copy.wait()
        qkv = dot(normed, wqkv_v[...])
        if layer + 1 < n_layers:
            for copy in qkv_copies(layer + 1):
                copy.start()
        cos_a, sin_a = cos_ref[...], sin_ref[...]

        def rotate(vec):
            return (vec * cos_a + pltpu.roll(vec, LANES // 2, 1) * sin_a).astype(BF16).astype(F32)

        for h in range(heads):
            qs[pl.ds(h, n_tok, stride=8), :] = rotate(qkv[:, h * LANES:(h + 1) * LANES])
        ktok[...] = rotate(qkv[:, q_cols:q_cols + LANES])
        vtok[...] = qkv[:, q_cols + LANES:q_cols + 2 * LANES].astype(BF16).astype(F32)
        k_mine = jnp.zeros((n_seq, LANES), F32)
        v_mine = jnp.zeros((n_seq, LANES), F32)
        for s in range(n_steps):
            mine = wsl_ref[s] >= 0
            k_mine = jnp.where(mine, ktok[pl.ds(s, n_seq, stride=n_steps), :], k_mine)
            v_mine = jnp.where(mine, vtok[pl.ds(s, n_seq, stride=n_steps), :], v_mine)
        ksel[...] = k_mine
        vsel[...] = v_mine
        ksel_out[layer] = k_mine
        vsel_out[layer] = v_mine
        if layer == 0:
            pl.semaphore_wait(barrier, n_sp)
        for copy in kv_copies(layer):
            copy.wait()

        def attend(b):
            slot = slot_ref[pl.ds(b, 1), :]
            here = lax.broadcasted_iota(jnp.int32, (LANES, LANES), 0) == slot
            keys = jnp.where(here, ksel[pl.ds(b, 1), :], k_v[layer, b].astype(F32)).astype(BF16)
            vals = jnp.where(here, vsel[pl.ds(b, 1), :], v_v[layer, b].astype(F32)).astype(BF16)
            rows = pl.ds(pl.multiple_of(b * 8 * n_steps, 8), 8 * n_steps)
            q = qs[rows, :].astype(BF16)
            scores = lax.dot_general(q, keys, (((1,), (1,)), ((), ())), preferred_element_type=F32) * LANES ** -0.5
            valid = lax.broadcasted_iota(jnp.int32, scores.shape, 1) <= limr[rows, :]
            scores = jnp.where(valid, scores, -1e30)
            top = jnp.max(scores, axis=-1, keepdims=True)
            w = jnp.exp(scores - top)
            total = jnp.sum(w, axis=-1, keepdims=True)
            o = dot(w.astype(BF16), vals)
            sub = lax.broadcasted_iota(jnp.int32, (8, LANES), 0)
            lane = lax.broadcasted_iota(jnp.int32, (8, LANES), 1)
            tiles = []
            for t in range(n_steps):
                part = slice(8 * t, 8 * t + 8)
                stat = jnp.where(lane == sub, top[part], jnp.where(lane == sub + LANES // 2, total[part], 0.0))
                stat = jnp.sum(stat, axis=0, keepdims=True)
                tiles.append(jnp.where(sub == heads, stat, o[part]))
            return tiles

        def seq_group(i, carry):
            group = []
            for k in range(SEQ_UNROLL):
                b = lax.rem(start_seq + i * SEQ_UNROLL + k, n_seq)
                group.append((b, attend(b)))
            for b, tiles in group:
                rows = pl.ds(pl.multiple_of(b * 8 * n_steps, 8), 8 * n_steps)
                send[layer, rows, :] = jnp.concatenate(tiles, axis=0)
            for b, tiles in group:
                for half in range(2):
                    dst = 2 * b + half
                    rows = pl.ds(pl.multiple_of(dst * 16, 16), 16)
                    home = pl.ds(pl.multiple_of(me * 16, 16), 16)

                    @pl.when(dst != me)
                    def _():
                        pltpu.make_async_remote_copy(
                            src_ref=send.at[layer, rows, :], dst_ref=recv.at[layer, home, :],
                            send_sem=rs_ss.at[layer], recv_sem=rs_rs.at[layer],
                            device_id=at_sp(dst), device_id_type=MESH).start()

                    @pl.when(dst == me)
                    def _():
                        recv[layer, home, :] = jnp.concatenate(tiles[2 * half:2 * half + 2], axis=0)
            return carry

        lax.fori_loop(0, n_seq // SEQ_UNROLL, seq_group, 0)
        peers = pl.ds(0, (n_sp - 1) * 16)
        rs_all = pltpu.make_async_remote_copy(
            src_ref=send.at[layer, peers, :], dst_ref=recv.at[layer, peers, :],
            send_sem=rs_ss.at[layer], recv_sem=rs_rs.at[layer], device_id=at_sp(me), device_id_type=MESH)
        rs_all.wait_recv()

        stats = jnp.concatenate([recv[layer, pl.ds(8 * t + heads, n_sp, stride=16), :] for t in range(2)], axis=0)
        stats = jnp.transpose(stats)
        tops, totals = stats[0:8], stats[LANES // 2:LANES // 2 + 8]
        for t in range(2):
            top_t = tops[:, t * n_sp:(t + 1) * n_sp]
            weight = jnp.exp(top_t - jnp.max(top_t, axis=-1, keepdims=True))
            denom = jnp.sum(weight * totals[:, t * n_sp:(t + 1) * n_sp], axis=-1, keepdims=True)
            numer = [jnp.zeros((8, LANES), F32) for _ in range(4)]
            for src in range(n_sp):
                numer[src % 4] = numer[src % 4] + weight[:, src:src + 1] * recv[layer, src * 16 + 8 * t:src * 16 + 8 * t + 8, :]
            merged = ((numer[0] + numer[1]) + (numer[2] + numer[3])) / denom
            for h in range(heads):
                pad_a[t:t + 1, h * LANES:(h + 1) * LANES] = merged[h:h + 1, :]

        wo_copy(layer).wait()
        part = dot(pad_a[...].astype(BF16), wo_v[...])[0:8]
        if layer + 1 < n_layers:
            wo_copy(layer + 1).start()
        u1 = (res[0:8, :] + exchange(layer, 0, part)).astype(BF16).astype(F32)
        h2 = rms_norm(jnp.concatenate([u1, jnp.zeros_like(u1)], axis=0), gm[layer:layer + 1, :])

        def gate_up(c, size):
            cols_copy(wg, wg_v, g_sem, layer, c, size).wait()
            cols_copy(wu, wu_v, u_sem, layer, c, size).wait()
            cols = pl.ds(pl.multiple_of(c * chunk, LANES), size)
            gate = dot(h2, wg_v[:, cols])
            up = dot(h2, wu_v[:, cols])
            g_v[:, cols] = (jax.nn.silu(gate) * up).astype(BF16)
            if layer + 1 < n_layers:
                cols_copy(wg, wg_v, g_sem, layer + 1, c, size).start()
                cols_copy(wu, wu_v, u_sem, layer + 1, c, size).start()

        def down(c, size):
            rows_copy(layer, c, size).wait()
            rows = pl.ds(pl.multiple_of(c * chunk, LANES), size)
            acc[...] += dot(g_v[:, rows], wd_v[rows, :])
            if layer + 1 < n_layers:
                rows_copy(layer + 1, c, size).start()

        def loop_of(piece):
            def step(c, carry):
                piece(c, chunk)
                return carry

            lax.fori_loop(0, n_full, step, 0)
            if tail:
                piece(n_full, tail)

        loop_of(gate_up)
        acc[...] = jnp.zeros_like(acc)
        loop_of(down)
        u2 = (u1 + exchange(layer, 1, acc[0:8, :])).astype(BF16).astype(F32)
        res[0:8, :] = u2

        row = jnp.where(core == 0, u2[0:1], u2[1:2])
        for j in range(blocks):
            ag[layer, j:j + 1, :] = row[:, j * LANES:(j + 1) * LANES]
        home = pl.ds(pl.multiple_of(me * 16, 16), blocks)
        ubuf[layer, core, home, :] = jnp.concatenate([row[:, j * LANES:(j + 1) * LANES] for j in range(blocks)], axis=0)

        def share(i, carry):
            dst = lax.rem(me + lax.rem(i + n_sp // 2, n_sp), n_sp)

            @pl.when(dst != me)
            def _():
                pltpu.make_async_remote_copy(
                    src_ref=ag.at[layer], dst_ref=ubuf.at[layer, core, home, :],
                    send_sem=ag_ss.at[layer], recv_sem=ag_rs.at[layer],
                    device_id=at_sp(dst), device_id_type=MESH).start()

            return carry

        lax.fori_loop(0, n_sp, share, 0)
        got = pl.ds(0, (n_sp - 1) * blocks)
        ag_all = pltpu.make_async_remote_copy(
            src_ref=ubuf.at[layer, core, got, :], dst_ref=ubuf.at[layer, core, got, :],
            send_sem=ag_ss.at[layer], recv_sem=ag_rs.at[layer], device_id=at_sp(me), device_id_type=MESH)
        ag_all.wait_recv()
        swap = pltpu.make_async_remote_copy(
            src_ref=ubuf.at[layer, core], dst_ref=ubuf.at[layer, core], send_sem=dd_ss.at[layer], recv_sem=dd_rs.at[layer],
            device_id={'tp': other}, device_id_type=MESH)
        swap.start()
        swap.wait()
        rs_all.wait_send()
        ag_all.wait_send()
        if layer + 1 < n_layers:
            for c in range(2):
                for j in range(blocks):
                    u3[j, pl.ds(c, n_sp, stride=2), :] = ubuf[layer, c, pl.ds(j, n_sp, stride=16), :]
        else:
            for s in range(n_steps):
                for j in range(blocks):
                    rows = pl.ds((s // 2) * 16 + j, n_seq, stride=32)
                    out[s, :, j * LANES:(j + 1) * LANES] = ubuf[layer, s % 2, rows, :].astype(BF16)


def solution(mesh):
    sp_size = mesh.shape['sp']
    dims = (4, 4, 4) if sp_size == 64 else (2, 2, 2)

    def local_fn(tok_emb, lengths, key_cache, val_cache, gain_attn, gain_mlp, w_query, w_key, w_value, w_out, w_gate, w_up, w_down):
        n_steps, n_seq, d_model = tok_emb.shape
        n_layers, _, loc_len, _, head_dim = key_cache.shape
        heads = w_query.shape[2] // head_dim
        ff = w_gate.shape[2]
        n_tok = n_steps * n_seq
        my_sp = lax.axis_index('sp')
        cur_pos = lengths[:, None] + jnp.arange(n_steps)[None, :]
        flat_pos = cur_pos.reshape(n_tok)
        half_dim = head_dim // 2
        inv_freq = 1.0 / (ROPE_BASE ** (jnp.arange(half_dim).astype(F32) * 2.0 / head_dim))
        angles = flat_pos.astype(F32)[:, None] * inv_freq[None, :]
        cos_h, sin_h = jnp.cos(angles), jnp.sin(angles)
        cos_a = jnp.concatenate([cos_h, cos_h], axis=-1)
        sin_a = jnp.concatenate([-sin_h, sin_h], axis=-1)
        lim = jnp.broadcast_to(jnp.floor_divide(flat_pos - my_sp, sp_size)[:, None], (n_tok, LANES)).astype(jnp.int32)
        wslot = jnp.where(cur_pos % sp_size == my_sp, cur_pos // sp_size, -1)
        slot = jnp.max(wslot, axis=1)
        wsl = jnp.broadcast_to(wslot.T[:, :, None], (n_steps, n_seq, LANES)).astype(jnp.int32)
        slot_b = jnp.broadcast_to(slot[:, None], (n_seq, LANES)).astype(jnp.int32)
        kc = key_cache.reshape(n_layers, n_seq, loc_len, head_dim)
        vc = val_cache.reshape(n_layers, n_seq, loc_len, head_dim)
        cfg = (dims, n_steps, n_layers, n_seq, heads, d_model, ff)
        blocks = d_model // LANES
        n_piece = -(-ff // min(MLP_CHUNK, ff))
        vm, hbm = pl.BlockSpec(memory_space=pltpu.VMEM), pl.BlockSpec(memory_space=pl.ANY)
        dma = pltpu.SemaphoreType.DMA
        hidden, k_new, v_new = pl.pallas_call(
            functools.partial(decode_kernel, cfg),
            out_shape=(
                jax.ShapeDtypeStruct((n_steps, n_seq, d_model), BF16),
                jax.ShapeDtypeStruct((n_layers, n_seq, LANES), F32),
                jax.ShapeDtypeStruct((n_layers, n_seq, LANES), F32),
            ),
            in_specs=[hbm] * 10 + [vm] * 7,
            out_specs=(vm, vm, vm),
            scratch_shapes=[
                pltpu.VMEM((n_steps, n_seq, d_model), BF16),
                pltpu.VMEM((n_layers, n_seq, loc_len, head_dim), BF16),
                pltpu.VMEM((n_layers, n_seq, loc_len, head_dim), BF16),
                pltpu.VMEM((d_model, (heads + 2) * LANES), BF16),
                pltpu.VMEM((heads * LANES, d_model), BF16),
                pltpu.VMEM((d_model, ff), BF16),
                pltpu.VMEM((d_model, ff), BF16),
                pltpu.VMEM((ff, d_model), BF16),
                pltpu.VMEM((blocks, n_tok, LANES), F32),
                pltpu.VMEM((8, LANES), F32),
                pltpu.VMEM((n_tok * 8, LANES), F32),
                pltpu.VMEM((n_tok * 8, LANES), jnp.int32),
                pltpu.VMEM((n_tok, LANES), F32),
                pltpu.VMEM((n_tok, LANES), F32),
                pltpu.VMEM((n_seq, LANES), F32),
                pltpu.VMEM((n_seq, LANES), F32),
                pltpu.VMEM((n_layers, n_tok * 8, LANES), F32),
                pltpu.VMEM((n_layers, n_tok * 8, LANES), F32),
                pltpu.VMEM((16, heads * LANES), F32),
                pltpu.VMEM((16, d_model), F32),
                pltpu.VMEM((16, ff), BF16),
                pltpu.VMEM((16, d_model), F32),
                pltpu.VMEM((n_layers, 2, 8, d_model), F32),
                pltpu.VMEM((n_layers, 2, 8, d_model), F32),
                pltpu.VMEM((n_layers, blocks, LANES), F32),
                pltpu.VMEM((n_layers, 2, sp_size * 16, LANES), F32),
                dma, dma((n_layers, 2)), dma((3,)), dma, dma((n_piece,)), dma((n_piece,)), dma((n_piece,)),
                dma((n_layers,)), dma((n_layers,)), dma((n_layers, 2)), dma((n_layers, 2)),
                dma((n_layers,)), dma((n_layers,)), dma((n_layers,)), dma((n_layers,)),
            ],
            compiler_params=pltpu.CompilerParams(collective_id=0, has_side_effects=True, vmem_limit_bytes=67043328),
        )(tok_emb, kc, vc, w_query, w_key, w_value, w_out, w_gate, w_up, w_down, cos_a, sin_a, lim, wsl, slot_b, gain_attn, gain_mlp)
        here = (jnp.arange(loc_len)[None, :] == slot[:, None])[None, :, :, None, None]
        new_keys = jnp.where(here, k_new.astype(BF16)[:, :, None, None, :], key_cache)
        new_vals = jnp.where(here, v_new.astype(BF16)[:, :, None, None, :], val_cache)
        return hidden, new_keys, new_vals

    cache_spec = P(None, 'dp', 'sp', 'tp', None)
    col_spec = P(None, None, 'tp')
    row_spec = P(None, 'tp', None)
    emb_spec = P(None, 'dp', None)
    return jax.shard_map(local_fn, mesh=mesh, in_specs=(emb_spec, P('dp'), cache_spec, cache_spec, P(), P(), col_spec, col_spec, col_spec, row_spec, col_spec, col_spec, row_spec), out_specs=(emb_spec, cache_spec, cache_spec), check_vma=False)
```

time: 2970 us -> 105 us (0.04)
  blocking collectives: 1470 us -> 0 us
  waiting for transfers between devices: 1100 us -> 0 us
  matrix products: 232 us -> 0 us
  Pallas kernels: 0 us -> 92 us
  local copies, waits for them, and re-layouts: 88.5 us -> 3.03 us
  other arithmetic: 44.1 us -> 8.75 us
    pmax x5 -> x0, blocking collectives: 1470 us -> none  [local_fn(): glob_max = lax.pmax(loc_max, 'sp')]
    psum x15 -> x0, waiting for transfers between devices: 1100 us -> none  [the longest x5 867 us: local_fn(): lax.psum(jnp.concatenate([loc_out, loc_sum], axis=-1) * rescale, 'sp')]
    dot_general x64 -> x0, matrix products: 232 us -> none  [the longest x48 201 us: project(): return jnp.dot(normed, weight, preferred_element_type=jnp.float32)]
    pallas_call x0 -> x1, Pallas kernels: none -> 92 us  [local_fn(): pl.pallas_call(functools.partial(decode_kernel, cfg), out_shape=(jax.Shap...]
    scatter x16 -> x0, local copies, waits for them, and re-layouts: 62.3 us -> none  [the longest x8 31.1 us: local_fn(): new_keys.at[layer_idx, row_ids, write_slot].set(k_rot, mode='drop')]
  transfers between devices with their start and end apart: 15 -> 0, of which waited for: 15 -> 0; matrix products, arithmetic and copies ran while one was open for 1% -> 0% of each run, Pallas kernels for 0% -> 0%
where the time goes in v1:
time: 105 us
  Pallas kernels  92 us (88%)
  other arithmetic  8.75 us (8%)
  local copies, waits for them, and re-layouts  3.03 us (3%)
    pallas_call x1, Pallas kernels, local_fn(): pl.pallas_call(functools.partial(decode_kernel, cfg), out_shape=(jax.Shap...  92 us
    select_n x1, other arithmetic, local_fn(): jnp.where(here, v_new.astype(BF16)[:, :, None, None, :], val_cache)  3.95 us

profile of v1, /device:TPU:1, one launch (start us, length us, event | category | flops | bytes accessed | tf_op | source)
XLA Modules:
  0.0 104.5 jit_solution(17789354963788868443)
XLA Ops:
  0.6 0.7 fusion.12
  1.3 0.9 fusion.3
  2.2 0.1 convert_element_type.24
  2.3 0.1 sub.29
  2.4 0.7 iota_compare_fusion
  3.1 0.7 broadcast_in_dim.34.slot_ref
  3.7 0.7 broadcast_in_dim.27.wsl_ref
  4.4 0.7 broadcast_in_dim.26.lim_ref
  5.1 0.3 fusion
  5.5 0.8 pad_maximum_fusion
  6.2 92.0 %shard_map.148 = (bf16[4,32,1536]{2,1,0:T(8,128)(2,1)}, f32[2,32,128]{2,1,0:T(8,128)}, f32[2,32,128]{2,1,0:T(8,128)}) custom-call(bf16[4,32,1536]{2,1,0:T(8,128)(2,1)} %emb.1, bf16[2,32,128,128]{3,2,1,0:T(8,128)(2,1)} %bitcast.2, bf16[2,32,128,128]{3,2,1,0:T(8,128)(2,1)} %bitcast.3, bf16[2,1536,768]{2,1,0:T(8,128)(2,1)} %wq.1, bf16[2,1536,128]{2,1,0:T(8,128)(2,1)} %wk.1, ...), custom_call_target="tpu_custom_call" | custom-call | tf_op jit(solution)/shard_map/pallas_call | solution.py:342
  98.3 0.8 convert_element_type.26
  99.0 0.8 convert_element_type.27
  99.8 0.0 copy-start
  99.8 4.0 %broadcast_select_fusion = (bf16[2,32,128,1,128]{4,2,3,1,0:T(8,128)(2,1)}, bf16[2,32,128,1,128]{4,2,3,1,0:T(8,128)(2,1)}) fusion(bf16[2,32,128,1,128]{4,2,3,1,0:T(8,128)(2,1)} %param.16, pred[32,128]{1,0:T(8,128)(4,1)} %iota_compare_fusion, bf16[2,32,128]{2,1,0:T(8,128)(2,1)S(1)} %convert_element_type.27, bf16[2,32,128,1,128]{4,2,3,1,0:T(8,128)(2,1)} %param.15, ...), kind=kLoop, calls=%fused_computation | loop fusion | flops 2097152 | bytes 8425472 | tf_op jit(solution)/shard_map/jit(_where)/select_n | solution.py:386
  103.8 0.0 copy-done
  103.8 0.7 copy.17
  (2 shorter events, 0.0 us)
Async XLA Ops:
  99.8 4.0 %copy-start = (bf16[4,32,1536]{2,1,0:T(8,128)(2,1)S(1)}, bf16[4,32,1536]{2,1,0:T(8,128)(2,1)}, u32[]{:S(2)}) copy-start(bf16[4,32,1536]{2,1,0:T(8,128)(2,1)} %get-tuple-element.22) | copy-start | bytes 1179652
